TPU v7x, 32 devices: a whole 2x2x4 slice. The times are simulated.
32 devices in a mesh: wide: 16 (over z, y, core), narrow: 2 (over x).
Axes of the slice: x: 2, y: 2, z: 4, core: 2. Of those that a mesh axis runs over, the one named last changes fastest.
Arguments:
- query_coords: float32 [3, 32, 16, 32], P(None, ('wide', 'narrow')), may hold values from -1 to 1
- owner_element: int32 [32, 16, 32], P(('wide', 'narrow')), may hold values from 0 to 15
- pair_counts: int32 [32, 32], P(('wide', 'narrow')), may hold values from 0 to 16, as said below
- fields: bfloat16 [512, 8, 1024], P(('wide', 'narrow')), may hold values from -6 to 6
Outputs:
- values: bfloat16 [16, 32, 16, 32], P(None, ('wide', 'narrow'))
Inputs may be any that keep to these rules, and one draw needn't show every extreme that they name: `pair_counts`: every count is at most 16, and some pair of devices reaches 16 in every draw.
All inputs are finite; a program needn't handle non-finite values.
Results may differ from a plain program's by a relative error of at most 0.0043.
Values may be sent and summed in bfloat16 or wider, within the bound.
No kernel may reach another device: no remote copies, remote signals or barrier semaphores. Data moves between devices by JAX's collectives and lax.ppermute only.
A program may use at most 64 MiB of HBM per device.

v0:
```python
import math
import jax
import jax.numpy as jnp
from jax import lax
from jax.sharding import PartitionSpec as P

GLL_NODES = (
    -1.0,
    -0.8717401485096066,
    -0.5917001814331423,
    -0.2092992179024789,
    0.2092992179024789,
    0.5917001814331423,
    0.8717401485096066,
    1.0,
)


def for_sending(shard):
    return jax.tree.map(lambda a: a.astype(jnp.bfloat16) if a.dtype == jnp.float32 else a, shard)


def lagrange(position):
    result = []
    for i in range(8):
        factor = jnp.ones_like(position)
        for m in range(8):
            if m != i:
                factor = factor * ((position - GLL_NODES[m]) / (GLL_NODES[i] - GLL_NODES[m]))
        result.append(factor)
    return jnp.stack(result)


def interpolate(payload, field_table):
    element_count = field_table.shape[0] // 8
    column_count = field_table.shape[1]
    half_cols = column_count // 2
    basis_r = lagrange(payload[0]).astype(jnp.bfloat16)
    tensor_st = (lagrange(payload[1])[:, None, :] * lagrange(payload[2])[None, :, :]).reshape(
        64, -1
    )
    picked = payload[3][None, :] == jnp.arange(element_count, dtype=jnp.float32)[:, None]
    weights = jnp.where(
        picked[:, None, :], basis_r[None, :, :], jnp.zeros((), jnp.bfloat16)
    ).reshape(element_count * 8, -1)
    halves = []
    for h in range(2):
        partial_value = lax.dot_general(
            field_table[:, h * half_cols : (h + 1) * half_cols],
            weights,
            (((0,), (0,)), ((), ())),
            preferred_element_type=jnp.float32,
        )
        halves.append(
            jnp.sum(partial_value.reshape(half_cols // 64, 64, -1) * tensor_st[None, :, :], axis=1)
        )
    return jnp.concatenate(halves, axis=0).astype(jnp.bfloat16)


def evaluate(payload, field_table):
    field_count = field_table.shape[1] // 64
    lead_shape = payload.shape[1:]
    flat = payload.reshape(4, -1)
    total_rows = flat.shape[1]
    block_rows = math.gcd(total_rows, 512)
    blocks = jnp.transpose(flat.reshape(4, total_rows // block_rows, block_rows), (1, 0, 2))

    def one_block(block):
        return interpolate(block, field_table)

    results = lax.map(one_block, blocks)
    return jnp.transpose(results, (1, 0, 2)).reshape((field_count,) + lead_shape)


def on_device(query_coords, owner_element, pair_counts, fields):
    wide_size = lax.axis_size("wide")
    narrow_size = lax.axis_size("narrow")
    device_count = wide_size * narrow_size
    slot_count = owner_element.shape[1]
    element_count = fields.shape[0]
    field_table = fields.reshape(element_count * fields.shape[1], fields.shape[2])
    live = jnp.arange(slot_count, dtype=jnp.int32)[:, None] < pair_counts[0][None, :]
    element_float = jnp.where(live, owner_element[0], element_count).astype(jnp.float32)
    payload = jnp.concatenate([query_coords[:, 0], element_float[None]], axis=0)
    payload = payload.reshape(4, slot_count, wide_size, narrow_size)
    arrived = lax.all_to_all(
        lax.all_to_all(payload, "wide", split_axis=2, concat_axis=2, tiled=True),
        "narrow",
        split_axis=3,
        concat_axis=3,
        tiled=True,
    )
    result = evaluate(arrived, field_table)
    returned = lax.all_to_all(
        lax.all_to_all(for_sending(result), "wide", split_axis=2, concat_axis=2, tiled=True),
        "narrow",
        split_axis=3,
        concat_axis=3,
        tiled=True,
    ).astype(result.dtype)
    return returned.reshape(returned.shape[0], 1, slot_count, device_count)


def solution(mesh):
    placed = (
        P(None, ("wide", "narrow"), None, None),
        P(("wide", "narrow"), None, None),
        P(("wide", "narrow"), None),
        P(("wide", "narrow"), None, None),
    )
    return jax.shard_map(
        on_device,
        mesh=mesh,
        in_specs=placed,
        out_specs=P(None, ("wide", "narrow"), None, None),
        check_vma=False,
    )
```

profile of v0, /device:TPU:0, one launch (start us, length us, event | category | flops | bytes accessed | tf_op | source)
XLA Modules:
  0.0 51.5 jit_solution(9558058476863743550)
XLA Ops:
  0.0 0.8 %copy.35 = s32[1,16,32]{1,2,0:T(8,128)S(1)} copy(s32[1,16,32]{2,1,0:T(8,128)} %param.5) | data formatting | bytes 4096 | tf_op args[1]
  0.9 0.7 %copy-done.2 = s32[1,32]{1,0:T(1,128)S(1)} copy-done((s32[1,32]{1,0:T(1,128)S(1)}, s32[1,32]{1,0:T(1,128)}, u32[]{:S(2)}) %copy-start.2) | copy-done | bytes 152
  1.8 13.7 %all_to_all.20 = f32[16,1,128]{2,1,0:T(1,128)S(1)} all-to-all(f32[16,1,128]{2,1,0:T(1,128)S(1)} %reshape.2410), channel_id=1, replica_groups=mesh['wide'=16,'narrow'=2] {'wide'}, dimensions={0} | all-to-all | bytes 16384 | tf_op jit(solution)/shard_map/all_to_all | solution.py:87
  15.4 0.5 broadcast.3145
  15.9 0.7 %reduce = f32[16,128]{1,0:T(8,128)S(1)} reduce(f32[16,1,128]{2,1,0:T(1,128)S(1)} %all_to_all.20, f32[]{:T(128)} %broadcast.3145), dimensions={1}, to_apply=%all_to_all.12.reduce_sub_computation | reduce | bytes 16388 | tf_op jit(solution)/shard_map/all_to_all | solution.py:87
  16.9 6.4 %all_to_all.21 = f32[2,1,1024]{2,1,0:T(1,128)S(1)} all-to-all(f32[2,1,1024]{2,1,0:T(1,128)S(1)} %reshape.2412), channel_id=1, replica_groups=mesh['wide'=16,'narrow'=2] {'narrow'}, dimensions={0} | all-to-all | bytes 16384 | tf_op jit(solution)/shard_map/all_to_all | solution.py:86
  23.2 0.7 %reduce.1 = f32[2,1024]{1,0:T(2,128)S(1)} reduce(f32[2,1,1024]{2,1,0:T(1,128)S(1)} %all_to_all.21, f32[]{:T(128)} %broadcast.3145), dimensions={1}, to_apply=%all_to_all.13.reduce_sub_computation | reduce | bytes 16388 | tf_op jit(solution)/shard_map/all_to_all | solution.py:86
  24.2 0.2 copy.38
  24.6 0.2 copy.57
  25.2 0.2 copy.56
  25.5 0.2 copy.62
  25.9 0.2 copy.54
  26.2 0.2 copy.46
  26.5 0.2 copy.45
  26.9 0.2 copy.44
  27.2 0.2 copy.43
  27.6 0.2 copy.42
  27.9 0.2 copy.41
  28.3 0.2 copy.39
  28.7 0.2 copy.40
  29.0 0.2 copy.53
  29.3 0.2 copy.52
  29.7 0.2 copy.51
  30.0 0.2 copy.50
  32.7 0.5 copy-done
  33.2 0.3 fusion
  33.5 0.4 multiply_reduce_fusion.1
  34.2 0.4 copy_bitcast_fusion.1
  34.8 9.1 %all_to_all.22 = bf16[16,2,256]{2,1,0:T(2,128)(2,1)S(1)} all-to-all(bf16[16,2,256]{2,1,0:T(2,128)(2,1)S(1)} %reshape.2414), channel_id=1, replica_groups=mesh['wide'=16,'narrow'=2] {'wide'}, dimensions={0} | all-to-all | bytes 32768 | tf_op jit(solution)/shard_map/all_to_all | solution.py:95
  44.2 6.2 %all_to_all.23 = bf16[2,2,2048]{2,1,0:T(2,128)(2,1)S(1)} all-to-all(bf16[2,2,2048]{2,1,0:T(2,128)(2,1)S(1)} %reshape.2416), channel_id=1, replica_groups=mesh['wide'=16,'narrow'=2] {'narrow'}, dimensions={0} | all-to-all | bytes 32768 | tf_op jit(solution)/shard_map/all_to_all | solution.py:94
  50.6 0.2 copy.67
  50.7 0.8 %copy.68 = bf16[16,1,16,32]{3,2,1,0:T(8,128)(2,1)} copy(bf16[16,1,16,32]{2,0,3,1:T(8,128)(2,1)S(1)} %bitcast.93) | data formatting | bytes 32768 | tf_op jit(solution)/shard_map/reshape | solution.py:101
  (59 shorter events, 7.0 us)
Async XLA Ops:
  0.0 0.8 %copy-start.1 = (f32[3,1,16,32]{3,2,1,0:T(8,128)S(1)}, f32[3,1,16,32]{3,2,1,0:T(8,128)}, u32[]{:S(2)}) copy-start(f32[3,1,16,32]{3,2,1,0:T(8,128)} %param.4) | copy-start | bytes 18436
  0.9 0.7 %copy-start.2 = (s32[1,32]{1,0:T(1,128)S(1)}, s32[1,32]{1,0:T(1,128)}, u32[]{:S(2)}) copy-start(s32[1,32]{1,0:T(1,128)} %param.6) | copy-start | bytes 388
  32.3 1.0 %copy-start = (bf16[16,8,1024]{2,1,0:T(8,128)(2,1)S(1)}, bf16[16,8,1024]{2,1,0:T(8,128)(2,1)}, u32[]{:S(2)}) copy-start(bf16[16,8,1024]{2,1,0:T(8,128)(2,1)} %param.7) | copy-start | bytes 786436
where the time goes:
time: 51.9 us; the launch traced here: 51.5 us
  blocking collectives  35.3 us (68%)
  local copies, waits for them, and re-layouts  13.2 us (25%)
  other arithmetic  2.05 us (4%)
  matrix products  0.69 us (1%)
    all_to_all x1, blocking collectives, on_device(): lax.all_to_all(payload, 'wide', split_axis=2, concat_axis=2, tiled=True)  13.7 us
    all_to_all x1, blocking collectives, on_device(): lax.all_to_all(for_sending(result), 'wide', split_axis=2, concat_axis=2,...  9.07 us
    all_to_all x1, blocking collectives, on_device(): lax.all_to_all(lax.all_to_all(payload, 'wide', split_axis=2, concat_axis=...  6.37 us
    all_to_all x1, blocking collectives, on_device(): lax.all_to_all(lax.all_to_all(for_sending(result), 'wide', split_axis=2,...  6.2 us
    mul x32, local copies, waits for them, and re-layouts, lagrange(): factor * ((position - GLL_NODES[m]) / (GLL_NODES[i] - GLL_NODES[m]))  5.1 us
    another operation x18, local copies, waits for them, and re-layouts  3.09 us
    unnamed x16, local copies, waits for them, and re-layouts  3.02 us

commit v1 on v0

--- a/solution.py
+++ b/solution.py
@@ -91,12 +91,22 @@
         tiled=True,
     )
     result = evaluate(arrived, field_table)
-    returned = lax.all_to_all(
-        lax.all_to_all(for_sending(result), "wide", split_axis=2, concat_axis=2, tiled=True),
-        "narrow",
-        split_axis=3,
-        concat_axis=3,
-        tiled=True,
+    returned = jnp.concatenate(
+        lax.all_to_all(
+            jnp.stack(
+                jnp.split(
+                    lax.all_to_all(
+                        for_sending(result), "wide", split_axis=2, concat_axis=2, tiled=True
+                    ),
+                    lax.axis_size("narrow"),
+                    axis=3,
+                )
+            ),
+            "narrow",
+            0,
+            0,
+        ),
+        axis=3,
     ).astype(result.dtype)
     return returned.reshape(returned.shape[0], 1, slot_count, device_count)
 

time: 51.9 us -> 52.5 us (1.012)
    another operation x18 -> x19, local copies, waits for them, and re-layouts: 3.09 us -> 3.89 us
    unnamed x16 -> x18, local copies, waits for them, and re-layouts: 3.02 us -> 3.33 us
where the time goes in v1:
time: 52.5 us; the launch traced here: 52.1 us
  blocking collectives  35.3 us (67%)
  local copies, waits for them, and re-layouts  13.7 us (26%)
  other arithmetic  2.08 us (4%)
  matrix products  0.69 us (1%)
    all_to_all x1, blocking collectives, on_device(): lax.all_to_all(payload, 'wide', split_axis=2, concat_axis=2, tiled=True)  13.7 us
    all_to_all x1, blocking collectives, on_device(): lax.all_to_all(for_sending(result), 'wide', split_axis=2, concat_axis=2,...  9.07 us
    all_to_all x1, blocking collectives, on_device(): lax.all_to_all(lax.all_to_all(payload, 'wide', split_axis=2, concat_axis=...  6.37 us
    all_to_all x1, blocking collectives, on_device(): lax.all_to_all(jnp.stack(jnp.split(lax.all_to_all(for_sending(result), 'w...  6.2 us
    mul x32, local copies, waits for them, and re-layouts, lagrange(): factor * ((position - GLL_NODES[m]) / (GLL_NODES[i] - GLL_NODES[m]))  5.1 us
    unnamed x18, local copies, waits for them, and re-layouts  3.33 us
    another operation x18, local copies, waits for them, and re-layouts  3.09 us

profile of v1, /device:TPU:0, one launch (start us, length us, event | category | flops | bytes accessed | tf_op | source)
XLA Modules:
  0.0 52.1 jit_solution(16606899599047046463)
XLA Ops:
  0.0 0.8 %copy.69 = s32[1,16,32]{1,2,0:T(8,128)S(1)} copy(s32[1,16,32]{2,1,0:T(8,128)} %param.5) | data formatting | bytes 4096 | tf_op args[1]
  0.9 0.7 %copy-done.2 = s32[1,32]{1,0:T(1,128)S(1)} copy-done((s32[1,32]{1,0:T(1,128)S(1)}, s32[1,32]{1,0:T(1,128)}, u32[]{:S(2)}) %copy-start.2) | copy-done | bytes 152
  1.8 13.7 %all_to_all.20 = f32[16,1,128]{2,1,0:T(1,128)S(1)} all-to-all(f32[16,1,128]{2,1,0:T(1,128)S(1)} %reshape.2410), channel_id=1, replica_groups=mesh['wide'=16,'narrow'=2] {'wide'}, dimensions={0} | all-to-all | bytes 16384 | tf_op jit(solution)/shard_map/all_to_all | solution.py:87
  15.4 0.5 broadcast.3145
  15.9 0.7 %reduce = f32[16,128]{1,0:T(8,128)S(1)} reduce(f32[16,1,128]{2,1,0:T(1,128)S(1)} %all_to_all.20, f32[]{:T(128)} %broadcast.3145), dimensions={1}, to_apply=%all_to_all.12.reduce_sub_computation | reduce | bytes 16388 | tf_op jit(solution)/shard_map/all_to_all | solution.py:87
  16.9 6.4 %all_to_all.21 = f32[2,1,1024]{2,1,0:T(1,128)S(1)} all-to-all(f32[2,1,1024]{2,1,0:T(1,128)S(1)} %reshape.2412), channel_id=1, replica_groups=mesh['wide'=16,'narrow'=2] {'narrow'}, dimensions={0} | all-to-all | bytes 16384 | tf_op jit(solution)/shard_map/all_to_all | solution.py:86
  23.2 0.7 %reduce.1 = f32[2,1024]{1,0:T(2,128)S(1)} reduce(f32[2,1,1024]{2,1,0:T(1,128)S(1)} %all_to_all.21, f32[]{:T(128)} %broadcast.3145), dimensions={1}, to_apply=%all_to_all.13.reduce_sub_computation | reduce | bytes 16388 | tf_op jit(solution)/shard_map/all_to_all | solution.py:86
  24.2 0.2 copy.72
  24.6 0.2 copy.91
  25.2 0.2 copy.90
  25.5 0.2 copy.96
  25.9 0.2 copy.88
  26.2 0.2 copy.80
  26.5 0.2 copy.79
  26.9 0.2 copy.78
  27.2 0.2 copy.77
  27.6 0.2 copy.76
  27.9 0.2 copy.75
  28.3 0.2 copy.73
  28.7 0.2 copy.74
  29.0 0.2 copy.87
  29.3 0.2 copy.86
  29.7 0.2 copy.85
  32.7 0.5 copy-done
  33.2 0.3 fusion
  33.5 0.4 multiply_reduce_fusion.1
  34.2 0.4 copy_bitcast_fusion
  34.8 9.1 %all_to_all.22 = bf16[16,2,256]{2,1,0:T(2,128)(2,1)S(1)} all-to-all(bf16[16,2,256]{2,1,0:T(2,128)(2,1)S(1)} %reshape.2414), channel_id=1, replica_groups=mesh['wide'=16,'narrow'=2] {'wide'}, dimensions={0} | all-to-all | bytes 32768 | tf_op jit(solution)/shard_map/all_to_all | solution.py:98
  44.0 0.2 fusion.16
  44.7 6.2 %all_to_all.23 = bf16[2,2,2048]{2,1,0:T(2,128)(2,1)S(1)} all-to-all(bf16[2,2,2048]{2,1,0:T(2,128)(2,1)S(1)} %reshape.2416), channel_id=1, replica_groups=mesh['wide'=16,'narrow'=2] {'narrow'}, dimensions={0} | all-to-all | bytes 32768 | tf_op jit(solution)/shard_map/all_to_all | solution.py:95
  51.1 0.3 copy.102
  51.3 0.8 %copy.103 = bf16[16,1,16,32]{3,2,1,0:T(8,128)(2,1)} copy(bf16[16,1,16,32]{2,0,3,1:T(8,128)(2,1)S(1)} %bitcast.95) | data formatting | bytes 32768 | tf_op jit(solution)/shard_map/reshape;reshape | solution.py:111
  (63 shorter events, 7.5 us)
Async XLA Ops:
  0.0 0.8 %copy-start.1 = (f32[3,1,16,32]{3,2,1,0:T(8,128)S(1)}, f32[3,1,16,32]{3,2,1,0:T(8,128)}, u32[]{:S(2)}) copy-start(f32[3,1,16,32]{3,2,1,0:T(8,128)} %param.4) | copy-start | bytes 18436
  0.9 0.7 %copy-start.2 = (s32[1,32]{1,0:T(1,128)S(1)}, s32[1,32]{1,0:T(1,128)}, u32[]{:S(2)}) copy-start(s32[1,32]{1,0:T(1,128)} %param.6) | copy-start | bytes 388
  32.3 1.0 %copy-start = (bf16[16,8,1024]{2,1,0:T(8,128)(2,1)S(1)}, bf16[16,8,1024]{2,1,0:T(8,128)(2,1)}, u32[]{:S(2)}) copy-start(bf16[16,8,1024]{2,1,0:T(8,128)(2,1)} %param.7) | copy-start | bytes 786436

commit v2 on v0

--- a/solution.py
+++ b/solution.py
@@ -92,7 +92,15 @@
     )
     result = evaluate(arrived, field_table)
     returned = lax.all_to_all(
-        lax.all_to_all(for_sending(result), "wide", split_axis=2, concat_axis=2, tiled=True),
+        jnp.concatenate(
+            lax.all_to_all(
+                jnp.stack(jnp.split(for_sending(result), lax.axis_size("wide"), axis=2)),
+                "wide",
+                0,
+                0,
+            ),
+            axis=2,
+        ),
         "narrow",
         split_axis=3,
         concat_axis=3,

time: 51.9 us -> 53.1 us (1.023)
  other arithmetic: 2.05 us -> 3.17 us
    unnamed x2 -> x16, other arithmetic: 0.4 us -> 1.43 us
where the time goes in v2:
time: 53.1 us; the launch traced here: 52.7 us
  blocking collectives  35.3 us (66%)
  local copies, waits for them, and re-layouts  13.2 us (25%)
  other arithmetic  3.17 us (6%)
  matrix products  0.69 us (1%)
    all_to_all x1, blocking collectives, on_device(): lax.all_to_all(payload, 'wide', split_axis=2, concat_axis=2, tiled=True)  13.7 us
    all_to_all x1, blocking collectives, on_device(): lax.all_to_all(jnp.stack(jnp.split(for_sending(result), lax.axis_size('wi...  9.07 us
    all_to_all x1, blocking collectives, on_device(): lax.all_to_all(lax.all_to_all(payload, 'wide', split_axis=2, concat_axis=...  6.37 us
    all_to_all x1, blocking collectives, on_device(): lax.all_to_all(jnp.concatenate(lax.all_to_all(jnp.stack(jnp.split(for_sen...  6.2 us
    mul x32, local copies, waits for them, and re-layouts, lagrange(): factor * ((position - GLL_NODES[m]) / (GLL_NODES[i] - GLL_NODES[m]))  5.1 us
    another operation x18, local copies, waits for them, and re-layouts  3.09 us
    unnamed x16, local copies, waits for them, and re-layouts  3.02 us
    unnamed x16, other arithmetic  1.43 us

profile of v2, /device:TPU:0, one launch (start us, length us, event | category | flops | bytes accessed | tf_op | source)
XLA Modules:
  0.0 52.7 jit_solution(2911857243344121557)
XLA Ops:
  0.0 0.8 %copy.66 = s32[1,16,32]{1,2,0:T(8,128)S(1)} copy(s32[1,16,32]{2,1,0:T(8,128)} %param.5) | data formatting | bytes 4096 | tf_op args[1]
  0.9 0.7 %copy-done.2 = s32[1,32]{1,0:T(1,128)S(1)} copy-done((s32[1,32]{1,0:T(1,128)S(1)}, s32[1,32]{1,0:T(1,128)}, u32[]{:S(2)}) %copy-start.2) | copy-done | bytes 152
  1.8 13.7 %all_to_all.20 = f32[16,1,128]{2,1,0:T(1,128)S(1)} all-to-all(f32[16,1,128]{2,1,0:T(1,128)S(1)} %reshape.2418), channel_id=1, replica_groups=mesh['wide'=16,'narrow'=2] {'wide'}, dimensions={0} | all-to-all | bytes 16384 | tf_op jit(solution)/shard_map/all_to_all | solution.py:87
  15.4 0.5 broadcast.3145
  15.9 0.7 %reduce = f32[16,128]{1,0:T(8,128)S(1)} reduce(f32[16,1,128]{2,1,0:T(1,128)S(1)} %all_to_all.20, f32[]{:T(128)} %broadcast.3145), dimensions={1}, to_apply=%all_to_all.12.reduce_sub_computation | reduce | bytes 16388 | tf_op jit(solution)/shard_map/all_to_all | solution.py:87
  16.9 6.4 %all_to_all.21 = f32[2,1,1024]{2,1,0:T(1,128)S(1)} all-to-all(f32[2,1,1024]{2,1,0:T(1,128)S(1)} %reshape.2420), channel_id=1, replica_groups=mesh['wide'=16,'narrow'=2] {'narrow'}, dimensions={0} | all-to-all | bytes 16384 | tf_op jit(solution)/shard_map/all_to_all | solution.py:86
  23.2 0.7 %reduce.1 = f32[2,1024]{1,0:T(2,128)S(1)} reduce(f32[2,1,1024]{2,1,0:T(1,128)S(1)} %all_to_all.21, f32[]{:T(128)} %broadcast.3145), dimensions={1}, to_apply=%all_to_all.13.reduce_sub_computation | reduce | bytes 16388 | tf_op jit(solution)/shard_map/all_to_all | solution.py:86
  24.2 0.2 copy.69
  24.6 0.2 copy.88
  25.2 0.2 copy.87
  25.5 0.2 copy.93
  25.9 0.2 copy.85
  26.2 0.2 copy.77
  26.5 0.2 copy.76
  26.9 0.2 copy.75
  27.2 0.2 copy.74
  27.6 0.2 copy.73
  27.9 0.2 copy.72
  28.3 0.2 copy.70
  28.7 0.2 copy.71
  29.0 0.2 copy.84
  29.3 0.2 copy.83
  29.7 0.2 copy.82
  30.0 0.2 copy.81
  30.3 0.2 copy.80
  30.6 0.2 copy.78
  32.7 0.5 copy-done
  33.2 0.3 fusion
  33.5 0.4 multiply_reduce_fusion.1
  35.9 9.1 %all_to_all.22 = bf16[16,2,256]{2,1,0:T(2,128)(2,1)S(1)} all-to-all(bf16[16,2,256]{2,1,0:T(2,128)(2,1)S(1)} %reshape.2422), channel_id=1, replica_groups=mesh['wide'=16,'narrow'=2] {'wide'}, dimensions={0} | all-to-all | bytes 32768 | tf_op jit(solution)/shard_map/all_to_all | solution.py:96
  45.4 6.2 %all_to_all.23 = bf16[2,2,2048]{2,1,0:T(2,128)(2,1)S(1)} all-to-all(bf16[2,2,2048]{2,1,0:T(2,128)(2,1)S(1)} %reshape.2424), channel_id=1, replica_groups=mesh['wide'=16,'narrow'=2] {'narrow'}, dimensions={0} | all-to-all | bytes 32768 | tf_op jit(solution)/shard_map/all_to_all | solution.py:94
  51.9 0.8 %copy.114 = bf16[16,1,16,32]{3,2,1,0:T(8,128)(2,1)} copy(bf16[16,1,16,32]{2,0,3,1:T(8,128)(2,1)S(1)} %bitcast.218) | data formatting | bytes 32768 | tf_op jit(solution)/shard_map/reshape | solution.py:109
  (75 shorter events, 8.3 us)
Async XLA Ops:
  0.0 0.8 %copy-start.1 = (f32[3,1,16,32]{3,2,1,0:T(8,128)S(1)}, f32[3,1,16,32]{3,2,1,0:T(8,128)}, u32[]{:S(2)}) copy-start(f32[3,1,16,32]{3,2,1,0:T(8,128)} %param.4) | copy-start | bytes 18436
  0.9 0.7 %copy-start.2 = (s32[1,32]{1,0:T(1,128)S(1)}, s32[1,32]{1,0:T(1,128)}, u32[]{:S(2)}) copy-start(s32[1,32]{1,0:T(1,128)} %param.6) | copy-start | bytes 388
  32.3 1.0 %copy-start = (bf16[16,8,1024]{2,1,0:T(8,128)(2,1)S(1)}, bf16[16,8,1024]{2,1,0:T(8,128)(2,1)}, u32[]{:S(2)}) copy-start(bf16[16,8,1024]{2,1,0:T(8,128)(2,1)} %param.7) | copy-start | bytes 786436
